TPU v7x, 128 devices: a whole 4x4x4 slice. The times are simulated.
128 devices in a mesh: slot: 32 (over x, z, y_hi), dp: 4 (over y_lo, core).
Axes of the slice: x: 4, y: 4 (y_hi: 2, y_lo: 2; y = y_hi * 2 + y_lo), z: 4, core: 2. Of those that a mesh axis runs over, the one named last changes fastest.
Arguments:
- tokens: bfloat16 [12, 4096, 1024], P('dp', 'slot'), may hold values from -6 to 6
- slot_keys: bfloat16 [1024, 1024], P(None, 'slot'), may hold values from -1.5 to 1.5
- expert_in: bfloat16 [128, 1024, 4096], P('slot', None, 'dp'), may hold values from -0.5 to 0.5
- expert_out: bfloat16 [128, 4096, 1024], P('slot', 'dp'), may hold values from -0.1875 to 0.1875
Outputs:
- combined: bfloat16 [12, 4096, 1024], P('dp', 'slot')
All inputs are finite; a program needn't handle non-finite values.
Results may differ from a plain program's by a relative error of at most 0.0085.
Values may be sent and summed in bfloat16 or wider, within the bound.
No kernel may reach another device: no remote copies, remote signals or barrier semaphores. Data moves between devices by JAX's collectives and lax.ppermute only.
A program may use at most 128 MiB of HBM per device.

v0:
```python
import jax
import jax.numpy as jnp
from jax import lax
from jax.sharding import Mesh
from jax.sharding import PartitionSpec as P

SLOT = ("slot_0", "slot_1", "slot_2")


def from_everyone(array, axis):
    copies = jnp.broadcast_to(array, (lax.axis_size(axis), *array.shape))
    return lax.all_to_all(copies, axis, split_axis=0, concat_axis=0, tiled=True)


def all_in_one(array, axis):
    leaves = jax.tree.leaves(array)
    turns = sorted(range(len(leaves)), key=lambda k: -leaves[k].size)
    width = (1, *leaves[turns[0]].shape)[-1]
    lines = [
        jnp.pad(leaves[k].reshape(-1), (0, -leaves[k].size % width)).reshape(-1, width)
        for k in turns
    ]
    both, at, found = (from_everyone(jnp.concatenate(lines), axis), 0, {})
    for k, line in zip(turns, lines):
        slab = both[:, at : at + len(line)].reshape(len(both), -1)
        found[k] = slab[:, : leaves[k].size].reshape(-1, *leaves[k].shape)
        at += len(line)
    numbers = iter(range(len(leaves)))
    return jax.tree.map(lambda _: found[next(numbers)], array)


def joined_by_halves(pieces, combine):
    while len(jax.tree.leaves(pieces)[0]) > 1:
        pieces = jax.vmap(combine)(
            *(jax.tree.map(lambda part: part[side::2], pieces) for side in (0, 1))
        )
    return jax.tree.map(lambda part: part[0], pieces)


def merged(array, axis, combine):
    pieces = all_in_one(array, axis)
    return joined_by_halves(pieces, combine)


def summed_rows(total, axes):
    for axis in axes:
        total = lax.psum_scatter(total, axis, scatter_dimension=0, tiled=True)
    return total


def laid_out(pieces, dim):
    pieces = jnp.moveaxis(pieces, 0, dim)
    lengths = pieces.shape
    return pieces.reshape(*lengths[:dim], lengths[dim] * lengths[dim + 1], *lengths[dim + 2 :])


def gathered_copies(array, axis, dim):
    pieces = from_everyone(array, axis)
    return laid_out(pieces, dim)


def cut_along(array, dim, size):
    before, after = (array.shape[:dim], array.shape[dim + 1 :])
    return jnp.moveaxis(array.reshape(*before, size, -1, *after), dim, 0)


def summed_on_arrival(array, axis, dim):
    pieces = cut_along(array, dim, lax.axis_size(axis))
    arrived = lax.all_to_all(pieces, axis, split_axis=0, concat_axis=0, tiled=True)
    return arrived.sum(axis=0)


def join_stats(first, second):
    highest = jnp.maximum(first[0], second[0])
    summed = first[1] * jnp.exp(first[0] - highest) + second[1] * jnp.exp(second[0] - highest)
    return (highest, summed)


def shards(tokens, slot_keys, expert_in, expert_out):
    images, positions, features = tokens.shape
    own_slots = slot_keys.shape[1]
    experts = expert_in.shape[0]
    per_expert = own_slots // experts
    all_keys = lax.all_gather(slot_keys, SLOT, axis=1, tiled=True)
    flat = tokens.reshape(images * positions, features)
    logits = jnp.dot(flat, all_keys, preferred_element_type=jnp.float32).reshape(
        images, positions, -1
    )
    local_peak = jnp.max(logits, axis=1)
    local_sum = jnp.sum(jnp.exp(logits - local_peak[:, None, :]), axis=1)
    peak, totals = merged((local_peak, local_sum), SLOT, join_stats)
    raised = jnp.exp(logits - peak[:, None, :])
    first_slot = lax.axis_index(SLOT) * own_slots
    own_totals = lax.dynamic_slice_in_dim(totals, first_slot, own_slots, 1)
    weights = raised.astype(jnp.bfloat16)
    summed = summed_rows(
        jnp.einsum("bms,bmd->sbd", weights, tokens, preferred_element_type=jnp.float32), SLOT
    )
    slot_inputs = (summed / own_totals.T[:, :, None]).astype(jnp.bfloat16)
    everyone = gathered_copies(slot_inputs, "dp", 1)
    length = images * lax.axis_size("dp")
    expert_rows = everyone.reshape(experts, per_expert * length, features)
    hidden = jnp.einsum("erd,edf->erf", expert_rows, expert_in, preferred_element_type=jnp.float32)
    hidden = jax.nn.gelu(hidden, approximate=True).astype(jnp.bfloat16)
    result = jnp.einsum("erf,efd->erd", hidden, expert_out, preferred_element_type=jnp.float32)
    slot_results = summed_on_arrival(
        jnp.transpose(result.reshape(own_slots, length, features), (1, 0, 2)), "dp", 0
    ).astype(jnp.bfloat16)
    mix = jax.nn.softmax(logits, axis=2).astype(jnp.bfloat16)
    combined = jnp.einsum(
        "bms,bsd->bmd",
        mix,
        lax.all_gather(slot_results, SLOT, axis=1, tiled=True),
        preferred_element_type=jnp.float32,
    )
    return combined.astype(jnp.bfloat16)


def solution(mesh):
    split = Mesh(
        mesh.devices.reshape(4, 4, 2, mesh.shape["dp"]), ("slot_0", "slot_1", "slot_2", "dp")
    )
    return jax.shard_map(
        shards,
        mesh=split,
        in_specs=(P("dp", SLOT, None), P(None, SLOT), P(SLOT, None, "dp"), P(SLOT, "dp", None)),
        out_specs=P("dp", SLOT, None),
        check_vma=False,
    )
```

profile of v0, /device:TPU:0, one launch (start us, length us, event | category | flops | bytes accessed | tf_op | source)
XLA Modules:
  0.0 450.6 jit_solution(11117423069919956325)
XLA Ops:
  6.5 0.0 copy-start
  6.5 0.0 all-gather.3.cloned.1.call-start
  6.5 0.7 all-gather.3.cloned.1.call-update
  7.3 0.0 reduce-scatter.4.cloned.1.call-start
  7.3 76.1 %all-gather.3.cloned.1.call-done = bf16[1024,1024]{0,1:T(8,128)(2,1)} async-done(((bf16[1024,32]{0,1:T(8,128)(2,1)}), bf16[1024,1024]{0,1:T(8,128)(2,1)}) %all-gather.3.cloned.1.call-update) | async-done | bytes 2097168 | tf_op jit(solution)/shard_map/all_gather | solution.py:84
  83.4 0.0 copy-done
  83.4 2.6 fusion.33
  86.0 0.2 exponential_reduce_fusion
  86.3 0.1 broadcast_in_dim.4
  86.4 21.6 %all_to_all.15 = f32[32,6,1024]{2,1,0:T(8,128)S(1)} all-to-all(f32[32,6,1024]{2,1,0:T(8,128)S(1)} %broadcast_in_dim.4), channel_id=1, replica_groups=mesh['slot_0'=4,'slot_1'=4,'slot_2'=2,'dp'=4] {'slot_0','slot_1','slot_2'}, dimensions={0} | all-to-all | bytes 1572864 | tf_op jit(solution)/shard_map/all_to_all | solution.py:12
  108.1 0.3 fusion.30
  108.4 0.2 multiply_add_fusion
  108.6 0.1 multiply_add_fusion.1
  108.7 0.1 multiply_add_fusion.2
  108.8 6.4 %convolution_bitcast_fusion = f32[1024,3,1024]{2,0,1:T(8,128)} fusion(bf16[3,128,1024]{2,1,0:T(8,128)(2,1)S(1)} %copy-done, f32[3,128,1024]{2,1,0:T(8,128)S(1)} %get-tuple-element.21, f32[3,1024]{1,0:T(4,128)S(1)} %bitcast.26), kind=kOutput, calls=%fused_computation.1 | convolution fusion | flops 806092800 | bytes 14954496 | tf_op jit(solution)/shard_map/bms,bmd->sbd/dot_general | solution.py:97
  115.2 0.0 reduce-scatter.4.cloned.1.call-update
  115.3 0.0 reduce-scatter.6.cloned.1.call-start
  115.3 110.5 %reduce-scatter.4.cloned.1.call-done = f32[256,3,1024]{2,0,1:T(8,128)} async-done(((f32[1024,3,1024]{2,0,1:T(8,128)}), f32[256,3,1024]{2,0,1:T(8,128)}) %reduce-scatter.4.cloned.1.call-update) | async-done | bytes 3145744 | tf_op jit(solution)/shard_map/reduce_scatter | solution.py:47
  225.8 0.0 reduce-scatter.6.cloned.1.call-update
  225.8 0.0 reduce-scatter.8.cloned.1.call-start
  225.9 40.6 %reduce-scatter.6.cloned.1.call-done = f32[64,3,1024]{2,0,1:T(8,128)} async-done(((f32[256,3,1024]{2,0,1:T(8,128)}), f32[64,3,1024]{2,0,1:T(8,128)}) %reduce-scatter.6.cloned.1.call-update) | async-done | bytes 786448 | tf_op jit(solution)/shard_map/reduce_scatter | solution.py:47
  266.5 0.0 reduce-scatter.8.cloned.1.call-update
  266.5 0.0 all-gather.5.cloned.1.call-start
  266.5 0.1 fusion.22
  266.6 23.2 %reduce-scatter.8.cloned.1.call-done = f32[32,3,1024]{2,0,1:T(8,128)} async-done(((f32[64,3,1024]{2,0,1:T(8,128)}), f32[32,3,1024]{2,0,1:T(8,128)}) %reduce-scatter.8.cloned.1.call-update) | async-done | bytes 393232 | tf_op jit(solution)/shard_map/reduce_scatter | solution.py:47
  289.9 1.1 divide_convert_fusion.2
  290.9 0.1 broadcast_in_dim.5
  291.0 14.0 %all_to_all.16 = bf16[4,32,3,1024]{3,1,2,0:T(8,128)(2,1)S(1)} all-to-all(bf16[4,32,3,1024]{3,1,2,0:T(8,128)(2,1)S(1)} %broadcast_in_dim.5), channel_id=1, replica_groups=mesh['slot_0'=4,'slot_1'=4,'slot_2'=2,'dp'=4] {'dp'}, dimensions={0} | all-to-all | bytes 1572864 | tf_op jit(solution)/shard_map/all_to_all | solution.py:12
  305.1 0.7 copy.11
  305.8 1.4 reshape_reshape.3
  307.2 10.0 %fusion.13 = f32[4,96,1024]{2,1,0:T(8,128)} fusion(bf16[4,1024,1024]{2,1,0:T(8,128)(2,1)} %param.7, bf16[4,96,1024]{2,1,0:T(8,128)(2,1)} %reshape_reshape.3, bf16[4,1024,1024]{2,1,0:T(8,128)(2,1)} %param.6), kind=kOutput, calls=%fused_computation.19 | convolution fusion | flops 1614151680 | bytes 19136512 | tf_op jit(solution)/shard_map/erf,efd->erd/dot_general | solution.py:105
  317.2 2.7 reshape.20
  319.9 2.5 copy.12
  322.4 23.2 %all_to_all.17 = f32[4,3,32,1024]{3,2,1,0:T(8,128)} all-to-all(f32[4,3,32,1024]{3,2,1,0:T(8,128)S(1)} %bitcast.24), channel_id=1, replica_groups=mesh['slot_0'=4,'slot_1'=4,'slot_2'=2,'dp'=4] {'dp'}, dimensions={0} | all-to-all | bytes 3145728 | tf_op jit(solution)/shard_map/all_to_all | solution.py:69
  345.6 2.2 reduce_sum.29
  347.9 0.0 all-gather.5.cloned.1.call-update
  347.9 0.4 fusion.34
  348.3 90.9 %all-gather.5.cloned.1.call-done = bf16[3,1024,1024]{2,1,0:T(8,128)(2,1)} async-done(((bf16[3,32,1024]{2,1,0:T(8,128)(2,1)}), bf16[3,1024,1024]{2,1,0:T(8,128)(2,1)}) %all-gather.5.cloned.1.call-update) | async-done | bytes 6291472 | tf_op jit(solution)/shard_map/all_gather | solution.py:113
  439.1 4.9 %convolution_convert_fusion = bf16[3,128,1024]{2,1,0:T(8,128)(2,1)} fusion(bf16[3,1024,1024]{2,1,0:T(8,128)(2,1)} %all-gather.5.cloned.1.call-done, f32[3,128]{1,0:T(4,128)S(1)} %fusion.34, f32[3,128,1024]{2,1,0:T(8,128)S(1)} %get-tuple-element.21), kind=kOutput, calls=%fused_computation.18 | convolution fusion | flops 806880640 | bytes 8652288 | tf_op jit(solution)/shard_map/bms,bsd->bmd/dot_general | solution.py:110
  (3 shorter events, 0.1 us)
Async XLA Ops:
  6.5 76.9 %copy-start = (bf16[3,128,1024]{2,1,0:T(8,128)(2,1)S(1)}, bf16[3,128,1024]{2,1,0:T(8,128)(2,1)}, u32[]{:S(2)}) copy-start(bf16[3,128,1024]{2,1,0:T(8,128)(2,1)} %param.4) | copy-start | bytes 2359300
  6.5 76.9 %all-gather.3.cloned.1.call-start = ((), (), s32[]{:S(2)}) async-start(), calls=%async_computation.6 | async-start | bytes 2162688 | tf_op jit(solution)/shard_map/all_gather | solution.py:84
  7.3 218.5 %reduce-scatter.4.cloned.1.call-start = ((), (), s32[]{:S(2)}) async-start(), calls=%async_computation.7 | async-start | bytes 15728640 | tf_op jit(solution)/shard_map/reduce_scatter | solution.py:47
  115.3 151.2 %reduce-scatter.6.cloned.1.call-start = ((), (), s32[]{:S(2)}) async-start(), calls=%async_computation.8 | async-start | bytes 3932160 | tf_op jit(solution)/shard_map/reduce_scatter | solution.py:47
  225.8 64.0 %reduce-scatter.8.cloned.1.call-start = ((), (), s32[]{:S(2)}) async-start(), calls=%async_computation.9 | async-start | bytes 1179648 | tf_op jit(solution)/shard_map/reduce_scatter | solution.py:47
  266.5 172.7 %all-gather.5.cloned.1.call-start = ((), (), s32[]{:S(2)}) async-start(), calls=%async_computation.10 | async-start | bytes 6488064 | tf_op jit(solution)/shard_map/all_gather | solution.py:113
Sparse Core Ops, SparseCore 0:
  10.3 73.0 all-gather.2
  115.4 110.3 reduce-scatter.3
  228.2 38.2 reduce-scatter.5
  268.7 21.1 reduce-scatter.7
  348.0 91.1 all-gather.4
where the time goes:
time: 451 us
  waiting for transfers between devices  342 us (76%)
  blocking collectives  58.9 us (13%)
  matrix products  24 us (5%)
  between operations  13.2 us (3%)
  local copies, waits for them, and re-layouts  7.76 us (2%)
    reduce_scatter x3, waiting for transfers between devices, summed_rows(): total = lax.psum_scatter(total, axis, scatter_dimension=0, tiled=True)  174 us
    all_gather x1, waiting for transfers between devices, shards(): lax.all_gather(slot_results, SLOT, axis=1, tiled=True)  90.9 us
    all_gather x1, waiting for transfers between devices, shards(): all_keys = lax.all_gather(slot_keys, SLOT, axis=1, tiled=True)  76.1 us
    all_to_all x2, blocking collectives, from_everyone(): return lax.all_to_all(copies, axis, split_axis=0, concat_axis=0, tiled=True)  35.7 us
    all_to_all x1, blocking collectives, summed_on_arrival(): lax.all_to_all(pieces, axis, split_axis=0, concat_axis=0, tiled=True)  23.2 us
    dot_general x1, matrix products, shards(): jnp.einsum('erf,efd->erd', hidden, expert_out, preferred_element_type=jnp...  10 us
  transfers between devices with their start and end apart: 5, of which 5 were waited for; matrix products, arithmetic and copies ran while one was open for 0% of the time, Pallas kernels for 0%

commit v1 on v0

--- a/solution.py
+++ b/solution.py
@@ -81,7 +81,9 @@
     own_slots = slot_keys.shape[1]
     experts = expert_in.shape[0]
     per_expert = own_slots // experts
-    all_keys = lax.all_gather(slot_keys, SLOT, axis=1, tiled=True)
+    all_keys = jnp.concatenate(
+        lax.all_to_all(jnp.stack([slot_keys] * lax.axis_size(SLOT)), SLOT, 0, 0), axis=1
+    )
     flat = tokens.reshape(images * positions, features)
     logits = jnp.dot(flat, all_keys, preferred_element_type=jnp.float32).reshape(
         images, positions, -1

time: 451 us -> 416 us (0.922)
  waiting for transfers between devices: 342 us -> 265 us
  blocking collectives: 58.9 us -> 101 us
    all_gather x1 -> x0, waiting for transfers between devices: 76.1 us -> none  [shards(): all_keys = lax.all_gather(slot_keys, SLOT, axis=1, tiled=True)]
    all_to_all x0 -> x1, blocking collectives: none -> 40.9 us  [shards(): lax.all_to_all(jnp.stack([slot_keys] * lax.axis_size(SLOT)), SLOT, 0, 0)]
  transfers between devices with their start and end apart: 5 -> 4, of which waited for: 5 -> 4; matrix products, arithmetic and copies ran while one was open for 0% -> 0% of each run, Pallas kernels for 0% -> 0%
where the time goes in v1:
time: 416 us
  waiting for transfers between devices  265 us (64%)
  blocking collectives  101 us (24%)
  matrix products  22.4 us (5%)
  between operations  13.2 us (3%)
  local copies, waits for them, and re-layouts  8.92 us (2%)
  other arithmetic  4.48 us (1%)
    reduce_scatter x3, waiting for transfers between devices, summed_rows(): total = lax.psum_scatter(total, axis, scatter_dimension=0, tiled=True)  174 us
    all_gather x1, waiting for transfers between devices, shards(): lax.all_gather(slot_results, SLOT, axis=1, tiled=True)  90.9 us
    all_to_all x1, blocking collectives, shards(): lax.all_to_all(jnp.stack([slot_keys] * lax.axis_size(SLOT)), SLOT, 0, 0)  40.9 us
    all_to_all x2, blocking collectives, from_everyone(): return lax.all_to_all(copies, axis, split_axis=0, concat_axis=0, tiled=True)  36.9 us
    all_to_all x1, blocking collectives, summed_on_arrival(): lax.all_to_all(pieces, axis, split_axis=0, concat_axis=0, tiled=True)  23.2 us
    dot_general x1, matrix products, shards(): jnp.einsum('erf,efd->erd', hidden, expert_out, preferred_element_type=jnp...  10 us
  transfers between devices with their start and end apart: 4, of which 4 were waited for; matrix products, arithmetic and copies ran while one was open for 0% of the time, Pallas kernels for 0%

profile of v1, /device:TPU:0, one launch (start us, length us, event | category | flops | bytes accessed | tf_op | source)
XLA Modules:
  0.0 415.5 jit_solution(696105563767812728)
XLA Ops:
  6.5 0.0 copy-start
  6.5 0.0 reduce-scatter.4.cloned.1.call-start
  6.5 1.2 stack.2
  7.7 40.9 %all_to_all.20 = bf16[32,1024,32]{1,2,0:T(8,128)(2,1)S(1)} all-to-all(bf16[32,1024,32]{1,2,0:T(8,128)(2,1)S(1)} %stack.2), channel_id=1, replica_groups=mesh['slot_0'=4,'slot_1'=4,'slot_2'=2,'dp'=4] {'slot_0','slot_1','slot_2'}, dimensions={0} | all-to-all | bytes 4194304 | tf_op jit(solution)/shard_map/all_to_all | solution.py:85
  48.6 0.0 copy-done
  48.6 1.1 fusion.31
  49.7 0.2 exponential_reduce_fusion
  50.0 0.1 broadcast_in_dim.4
  50.1 22.8 %all_to_all.21 = f32[32,6,1024]{2,1,0:T(8,128)S(1)} all-to-all(f32[32,6,1024]{2,1,0:T(8,128)S(1)} %broadcast_in_dim.4), channel_id=1, replica_groups=mesh['slot_0'=4,'slot_1'=4,'slot_2'=2,'dp'=4] {'slot_0','slot_1','slot_2'}, dimensions={0} | all-to-all | bytes 1572864 | tf_op jit(solution)/shard_map/all_to_all | solution.py:12
  72.9 0.3 fusion.28
  73.2 0.2 multiply_add_fusion
  73.4 0.1 multiply_add_fusion.1
  73.5 0.1 multiply_add_fusion.2
  73.7 6.4 %convolution_bitcast_fusion = f32[1024,3,1024]{2,0,1:T(8,128)} fusion(bf16[3,128,1024]{2,1,0:T(8,128)(2,1)S(1)} %copy-done, f32[3,128,1024]{2,1,0:T(8,128)S(1)} %get-tuple-element.21, f32[3,1024]{1,0:T(4,128)S(1)} %bitcast.28), kind=kOutput, calls=%fused_computation.1 | convolution fusion | flops 806092800 | bytes 14954496 | tf_op jit(solution)/shard_map/bms,bmd->sbd/dot_general | solution.py:99
  80.1 0.0 reduce-scatter.4.cloned.1.call-update
  80.1 0.0 reduce-scatter.6.cloned.1.call-start
  80.2 110.4 %reduce-scatter.4.cloned.1.call-done = f32[256,3,1024]{2,0,1:T(8,128)} async-done(((f32[1024,3,1024]{2,0,1:T(8,128)}), f32[256,3,1024]{2,0,1:T(8,128)}) %reduce-scatter.4.cloned.1.call-update) | async-done | bytes 3145744 | tf_op jit(solution)/shard_map/reduce_scatter | solution.py:47
  190.6 0.0 reduce-scatter.6.cloned.1.call-update
  190.6 0.0 reduce-scatter.8.cloned.1.call-start
  190.6 40.6 %reduce-scatter.6.cloned.1.call-done = f32[64,3,1024]{2,0,1:T(8,128)} async-done(((f32[256,3,1024]{2,0,1:T(8,128)}), f32[64,3,1024]{2,0,1:T(8,128)}) %reduce-scatter.6.cloned.1.call-update) | async-done | bytes 786448 | tf_op jit(solution)/shard_map/reduce_scatter | solution.py:47
  231.3 0.0 reduce-scatter.8.cloned.1.call-update
  231.3 0.0 all-gather.2.cloned.1.call-start
  231.3 0.1 fusion.20
  231.4 23.4 %reduce-scatter.8.cloned.1.call-done = f32[32,3,1024]{2,0,1:T(8,128)} async-done(((f32[64,3,1024]{2,0,1:T(8,128)}), f32[32,3,1024]{2,0,1:T(8,128)}) %reduce-scatter.8.cloned.1.call-update) | async-done | bytes 393232 | tf_op jit(solution)/shard_map/reduce_scatter | solution.py:47
  254.8 1.1 divide_convert_fusion.2
  255.9 0.1 broadcast_in_dim.5
  256.0 14.0 %all_to_all.22 = bf16[4,32,3,1024]{3,1,2,0:T(8,128)(2,1)S(1)} all-to-all(bf16[4,32,3,1024]{3,1,2,0:T(8,128)(2,1)S(1)} %broadcast_in_dim.5), channel_id=1, replica_groups=mesh['slot_0'=4,'slot_1'=4,'slot_2'=2,'dp'=4] {'dp'}, dimensions={0} | all-to-all | bytes 1572864 | tf_op jit(solution)/shard_map/all_to_all | solution.py:12
  270.0 0.7 copy.14
  270.7 1.4 reshape_reshape.3
  272.1 10.0 %fusion.11 = f32[4,96,1024]{2,1,0:T(8,128)} fusion(bf16[4,1024,1024]{2,1,0:T(8,128)(2,1)} %param.7, bf16[4,96,1024]{2,1,0:T(8,128)(2,1)} %reshape_reshape.3, bf16[4,1024,1024]{2,1,0:T(8,128)(2,1)} %param.6), kind=kOutput, calls=%fused_computation.17 | convolution fusion | flops 1614151680 | bytes 19136512 | tf_op jit(solution)/shard_map/erf,efd->erd/dot_general | solution.py:107
  282.2 2.7 reshape.30
  284.8 2.5 copy.15
  287.3 23.2 %all_to_all.23 = f32[4,3,32,1024]{3,2,1,0:T(8,128)} all-to-all(f32[4,3,32,1024]{3,2,1,0:T(8,128)S(1)} %bitcast.25), channel_id=1, replica_groups=mesh['slot_0'=4,'slot_1'=4,'slot_2'=2,'dp'=4] {'dp'}, dimensions={0} | all-to-all | bytes 3145728 | tf_op jit(solution)/shard_map/all_to_all | solution.py:69
  310.6 2.2 reduce_sum.29
  312.8 0.0 all-gather.2.cloned.1.call-update
  312.8 0.4 fusion.32
  313.2 90.9 %all-gather.2.cloned.1.call-done = bf16[3,1024,1024]{2,1,0:T(8,128)(2,1)} async-done(((bf16[3,32,1024]{2,1,0:T(8,128)(2,1)}), bf16[3,1024,1024]{2,1,0:T(8,128)(2,1)}) %all-gather.2.cloned.1.call-update) | async-done | bytes 6291472 | tf_op jit(solution)/shard_map/all_gather | solution.py:115
  404.1 4.9 %convolution_convert_fusion = bf16[3,128,1024]{2,1,0:T(8,128)(2,1)} fusion(bf16[3,1024,1024]{2,1,0:T(8,128)(2,1)} %all-gather.2.cloned.1.call-done, f32[3,128]{1,0:T(4,128)S(1)} %fusion.32, f32[3,128,1024]{2,1,0:T(8,128)S(1)} %get-tuple-element.21), kind=kOutput, calls=%fused_computation.16 | convolution fusion | flops 806880640 | bytes 8652288 | tf_op jit(solution)/shard_map/bms,bsd->bmd/dot_general | solution.py:112
  (3 shorter events, 0.1 us)
Async XLA Ops:
  6.5 42.1 %copy-start = (bf16[3,128,1024]{2,1,0:T(8,128)(2,1)S(1)}, bf16[3,128,1024]{2,1,0:T(8,128)(2,1)}, u32[]{:S(2)}) copy-start(bf16[3,128,1024]{2,1,0:T(8,128)(2,1)} %param.4) | copy-start | bytes 2359300
  6.5 184.0 %reduce-scatter.4.cloned.1.call-start = ((), (), s32[]{:S(2)}) async-start(), calls=%async_computation.7 | async-start | bytes 15728640 | tf_op jit(solution)/shard_map/reduce_scatter | solution.py:47
  80.1 151.2 %reduce-scatter.6.cloned.1.call-start = ((), (), s32[]{:S(2)}) async-start(), calls=%async_computation.8 | async-start | bytes 3932160 | tf_op jit(solution)/shard_map/reduce_scatter | solution.py:47
  190.6 64.2 %reduce-scatter.8.cloned.1.call-start = ((), (), s32[]{:S(2)}) async-start(), calls=%async_computation.9 | async-start | bytes 1179648 | tf_op jit(solution)/shard_map/reduce_scatter | solution.py:47
  231.3 172.8 %all-gather.2.cloned.1.call-start = ((), (), s32[]{:S(2)}) async-start(), calls=%async_computation.10 | async-start | bytes 6488064 | tf_op jit(solution)/shard_map/all_gather | solution.py:115
Sparse Core Ops, SparseCore 0:
  80.2 110.3 reduce-scatter.3
  193.0 38.2 reduce-scatter.5
  233.6 21.1 reduce-scatter.7
  312.9 91.1 all-gather.1
